TPU v7x, 32 devices: a whole 2x2x4 slice. The times are simulated.
32 devices in a mesh: row: 2 (over core), col: 4 (over y, x), depth: 4 (over z).
Axes of the slice: x: 2, y: 2, z: 4, core: 2. Of those that a mesh axis runs over, the one named last changes fastest.
Arguments:
- a_tile: float32 [2048, 2048], P('row', 'col'), as said below
- panels: float32 [2048, 4096], P('row', 'depth'), as said below
Outputs:
- trailing: float32 [2048, 2048], P(('row', 'depth'), 'col')
- new_panel: float32 [2048, 512], P(('row', 'col'))
- diag_norm: float32 [1], replicated
Inputs may be any that keep to these rules, and one draw needn't show every extreme that they name: symmetric; a_tile - panels panels^T is positive definite with a large positive diagonal. `panels`: real-valued entries of full rank.
All inputs are finite; a program needn't handle non-finite values.
Results may differ from a plain program's by a relative error of at most 0.00015.
Values sent between devices are 32-bit elements; how exact they have to be, the bound alone decides.
A program may use at most 64 MiB of HBM per device.

v0:
```python
import jax
import jax.numpy as jnp
from jax import lax
from jax.sharding import PartitionSpec as P

PB = 512


def from_root(value, axis, source):
    kept = jnp.where(lax.axis_index(axis) == source, value, 0).astype(value.dtype)
    return lax.psum(kept, axis)


def outer_rows(left, right):
    return lax.dot_general(
        left,
        right,
        (((1,), (1,)), ((), ())),
        precision=lax.Precision.HIGHEST,
        preferred_element_type=jnp.float32,
    )


def local(a_tile, panels):
    tile_rows, tile_cols = a_tile.shape
    depth_count = lax.axis_size("depth")
    row_index = lax.axis_index("row")
    col_index = lax.axis_index("col")
    depth_index = lax.axis_index("depth")
    first = col_index * tile_cols
    every_row = lax.all_gather(panels, "row", axis=0, tiled=True)
    col_panels = lax.dynamic_slice_in_dim(every_row, first, tile_cols, 0)
    keep_base = depth_index == 0
    share_rows = tile_rows // depth_count
    trailing = lax.psum_scatter(
        jnp.where(keep_base, a_tile, 0.0) - outer_rows(panels, col_panels),
        "depth",
        scatter_dimension=0,
        tiled=True,
    )
    panel_block = lax.all_gather(trailing, "depth", axis=0, tiled=True)
    diag_block = from_root(panel_block[:PB], "row", 0)
    factor = jnp.linalg.cholesky(diag_block)
    solved = jax.scipy.linalg.solve_triangular(factor, panel_block.T, lower=True).T
    col_share = tile_rows // lax.axis_size("col")
    received = lax.all_to_all(solved, "col", split_axis=0, concat_axis=0, tiled=True)
    new_panel = received[:col_share]
    rows_global = (
        row_index * tile_rows
        + depth_index * share_rows
        + jnp.arange(share_rows, dtype=jnp.int32)[:, None]
    )
    cols_global = first + jnp.arange(tile_cols, dtype=jnp.int32)[None, :]
    squares = jnp.sum(jnp.where(rows_global == cols_global, trailing * trailing, 0.0))
    total = lax.psum(squares, ("row", "col", "depth"))
    order = tile_cols * lax.axis_size("col")
    diag_norm = jnp.sqrt(total / order).reshape(1)
    return (trailing, new_panel, diag_norm)


def solution(mesh):
    return jax.shard_map(
        local,
        mesh=mesh,
        in_specs=(P("row", "col"), P("row", "depth")),
        out_specs=(P(("row", "depth"), "col"), P(("row", "col"), None), P()),
        check_vma=False,
    )
```

profile of v0, /device:TPU:0, one launch (start us, length us, event | category | flops | bytes accessed | tf_op | source)
XLA Modules:
  0.0 379.0 jit_solution(3016540084601054819)
XLA Ops:
  7.2 0.7 all-gather.3.cloned.1.call-update
  7.9 1.9 copy.5
  9.9 22.2 %all-gather.3.cloned.1.call-done = f32[2048,1024]{1,0:T(8,128)} async-done(((f32[1024,1024]{1,0:T(8,128)}), f32[2048,1024]{1,0:T(8,128)}) %all-gather.3.cloned.1.call-update) | async-done | bytes 8388624 | tf_op jit(solution)/shard_map/all_gather | solution.py:31
  32.1 10.4 %bitcast_subtract_fusion = f32[1024,512]{0,1:T(8,128)} fusion(f32[1024,512]{0,1:T(8,128)S(1)} %copy.5, f32[1024,1024]{1,0:T(8,128)} %param.3, f32[2048,1024]{1,0:T(8,128)} %all-gather.3.cloned.1.call-done, s32[]{:T(128)S(6)} %select_n.29, pred[]{:T(512)S(6)} %eq.19), kind=kOutput, calls=%fused_computation.3 | convolution fusion | flops 6443499520 | bytes 10485765 | tf_op jit(solution)/shard_map/dot_general | solution.py:15
  42.6 44.9 %reduce-scatter.2.cloned.1.call-done = f32[256,512]{0,1:T(8,128)} async-done(((f32[1024,512]{0,1:T(8,128)}), f32[256,512]{0,1:T(8,128)}) %reduce-scatter.2.cloned.1.call-update) | async-done | bytes 524304 | tf_op jit(solution)/shard_map/reduce_scatter | solution.py:35
  87.5 0.5 all-reduce.3.cloned.1.call-start
  88.0 45.9 %all-gather.5.cloned.1.call-done = f32[1024,512]{0,1:T(8,128)} async-done(((f32[256,512]{0,1:T(8,128)}), f32[1024,512]{0,1:T(8,128)}) %all-gather.5.cloned.1.call-update) | async-done | bytes 2097168 | tf_op jit(solution)/shard_map/all_gather | solution.py:41
  133.9 2.3 slice_select_fusion
  136.3 18.4 %all-reduce.3.cloned.1.call-done = f32[512,512]{0,1:T(8,128)} async-done(((f32[512,512]{0,1:T(8,128)}), f32[512,512]{0,1:T(8,128)}) %all-reduce.3.cloned.1.call-update) | async-done | bytes 1048592 | tf_op jit(solution)/shard_map/psum | solution.py:11
  154.6 1.6 copy.6
  156.3 0.2 fusion.16
  156.6 11.7 %cholesky.103 = f32[128,128]{1,0:T(8,128)S(1)} custom-call(f32[128,128]{1,0:T(8,128)S(1)} %cholesky.263), custom_call_target="Cholesky" | custom-call | tf_op jit(solution)/shard_map/jit(cholesky)/cholesky | solution.py:43
  168.3 0.1 copy.7
  168.4 9.8 %custom-call.31 = f32[1,128,128]{1,2,0:T(8,128)S(1)} custom-call(f32[1,128,128]{2,1,0:T(8,128)S(1)} %get-tuple-element.33), custom_call_target="InvertDiagBlocksLowerTriangular" | custom-call | tf_op jit(solution)/shard_map/jit(cholesky)/cholesky | solution.py:43
  178.2 0.3 fusion.22
  178.5 0.1 copy.8
  178.7 0.3 convolution_subtract_fusion.2
  179.0 11.7 %cholesky.215 = f32[128,128]{1,0:T(8,128)S(1)} custom-call(f32[128,128]{1,0:T(8,128)S(1)} %cholesky.267), custom_call_target="Cholesky" | custom-call | tf_op jit(solution)/shard_map/jit(cholesky)/cholesky | solution.py:43
  190.7 0.1 copy.9
  190.9 10.0 %custom-call.32 = f32[1,128,128]{1,2,0:T(8,128)S(1)} custom-call(f32[1,128,128]{2,1,0:T(8,128)S(1)} %get-tuple-element.31), custom_call_target="InvertDiagBlocksLowerTriangular" | custom-call | tf_op jit(solution)/shard_map/jit(cholesky)/cholesky | solution.py:43
  200.8 0.1 cholesky.222
  201.0 0.3 convolution_dynamic-update-slice_fusion
  201.3 1.5 convolution_subtract_fusion.3
  202.8 11.7 %cholesky.236 = f32[128,128]{1,0:T(8,128)S(1)} custom-call(f32[128,128]{1,0:T(8,128)S(1)} %cholesky.272), custom_call_target="Cholesky" | custom-call | tf_op jit(solution)/shard_map/jit(cholesky)/cholesky | solution.py:43
  214.6 0.1 copy.11
  214.7 9.8 %custom-call.33 = f32[1,128,128]{1,2,0:T(8,128)S(1)} custom-call(f32[1,128,128]{2,1,0:T(8,128)S(1)} %get-tuple-element.29), custom_call_target="InvertDiagBlocksLowerTriangular" | custom-call | tf_op jit(solution)/shard_map/jit(cholesky)/cholesky | solution.py:43
  224.5 0.3 convolution_dynamic-update-slice_fusion.1
  224.8 1.3 convolution_subtract_fusion.4
  226.2 11.9 %cholesky.253 = f32[128,128]{1,0:T(8,128)S(1)} custom-call(f32[128,128]{1,0:T(8,128)S(1)} %convolution_subtract_fusion.4), custom_call_target="Cholesky" | custom-call | tf_op jit(solution)/shard_map/jit(cholesky)/cholesky | solution.py:43
  238.0 0.1 copy.13
  238.2 0.6 compare_reduce_fusion.1
  238.8 0.7 compare_reduce_fusion
  239.5 0.6 compare_reduce_fusion.2
  242.7 1.1 select_select_fusion
  243.8 12.0 %while.1 = (s32[]{:T(128)}, f32[512,512]{0,1:T(8,128)}, s32[4,2]{0,1:T(2,128)S(1)}, f32[4,128,128]{2,1,0:T(8,128)S(1)}, s32[]{:T(128)}) while((s32[]{:T(128)}, f32[512,512]{0,1:T(8,128)}, s32[4,2]{0,1:T(2,128)S(1)}, f32[4,128,128]{2,1,0:T(8,128)S(1)}, s32[]{:T(128)}) %tuple.29), condition=%wide.while_cond, body=%wide.while_body.sunk | while | flops 2 | bytes 393329 | solution.py:44
  243.8 0.1 constant_dynamic-slice_fusion.2
  243.9 0.5 fusion.47
  244.4 2.3 dynamic-slice.7
  246.7 0.1 copy.22
  246.9 0.5 fusion.47
  247.4 2.3 dynamic-slice.7
  249.7 0.1 copy.22
  249.9 0.5 fusion.47
  250.4 2.3 dynamic-slice.7
  252.7 0.1 copy.22
  252.9 0.1 constant_dynamic-slice_fusion.2
  252.9 0.5 fusion.47
  253.5 2.2 dynamic-slice.7
  255.7 0.1 copy.22
  255.8 39.3 %custom-call.34 = f32[4,128,128]{1,2,0:T(8,128)S(1)} custom-call(f32[4,128,128]{2,1,0:T(8,128)S(1)} %get-tuple-element.10), custom_call_target="InvertDiagBlocksLowerTriangular" | custom-call | tf_op jit(solution)/shard_map/jit(_solve_triangular)/triangular_solve | solution.py:44
  295.2 0.6 fusion.17
  295.8 1.5 convolution_subtract_fusion.1
  297.3 0.6 fusion.30
  297.9 1.6 convolution_subtract_fusion
  299.5 0.6 fusion.28
  300.2 2.0 fusion.10
  302.2 0.6 fusion.27
  302.9 0.1 maximum_bitcast_fusion
  303.0 1.9 copy.19
  304.9 4.1 %all-to-all-start = ((f32[4,256,512]{2,1,0:T(8,128)}), f32[4,256,512]{2,1,0:T(8,128)S(1)}, u32[]{:S(2)}, u32[]{:S(2)}) async-start(f32[4,256,512]{2,1,0:T(8,128)} %bitcast.14), calls=%async_computation.1 | async-start | bytes 4194304 | tf_op jit(solution)/shard_map/all_to_all | solution.py:46
  309.0 0.8 select_reduce_fusion
  309.8 58.8 %psum.15 = f32[]{:T(128)} all-reduce(f32[]{:T(128)} %select_reduce_fusion), channel_id=1, replica_groups=mesh['row'=2,'col'=4,'depth'=4] {'row','col','depth'}, use_global_device_ids=true, to_apply=%region_11.12 | all-reduce | flops 1 | bytes 8 | tf_op jit(solution)/shard_map/psum | solution.py:55
  369.2 1.0 copy.16
  370.2 0.8 slice_bitcast_fusion
  (37 shorter events, 0.6 us)
Async XLA Ops:
  7.2 25.0 %all-gather.3.cloned.1.call-start = ((), (), s32[]{:S(2)}) async-start(), calls=%async_computation.2 | async-start | bytes 12582912 | tf_op jit(solution)/shard_map/all_gather | solution.py:31
  7.9 79.6 %reduce-scatter.2.cloned.1.call-start = ((), (), s32[]{:S(2)}) async-start(), calls=%async_computation.3 | async-start | bytes 2621440 | tf_op jit(solution)/shard_map/reduce_scatter | solution.py:35
  42.5 91.4 %all-gather.5.cloned.1.call-start = ((), (), s32[]{:S(2)}) async-start(), calls=%async_computation.4 | async-start | bytes 2621440 | tf_op jit(solution)/shard_map/all_gather | solution.py:41
  87.5 67.1 %all-reduce.3.cloned.1.call-start = ((), (), s32[]{:S(2)}) async-start(), calls=%async_computation.5 | async-start | bytes 2097152 | tf_op jit(solution)/shard_map/psum | solution.py:11
  154.6 1.7 copy-start.2
  156.5 34.4 %copy-start.3 = (f32[512,512]{1,0:T(8,128)}, f32[512,512]{1,0:T(8,128)S(1)}, u32[]{:S(2)}) copy-start(f32[512,512]{1,0:T(8,128)S(1)} %fusion.16) | copy-start | bytes 3145732
  242.7 52.5 %copy-start = (f32[1024,512]{0,1:T(8,128)S(1)}, f32[1024,512]{0,1:T(8,128)}, u32[]{:S(2)}) copy-start(f32[1024,512]{0,1:T(8,128)} %all-gather.5.cloned.1.call-done) | copy-start | bytes 6291460
  304.9 4.1 %copy-start.1 = (f32[256,512]{0,1:T(8,128)S(1)}, f32[256,512]{0,1:T(8,128)}, u32[]{:S(2)}) copy-start(f32[256,512]{0,1:T(8,128)} %reduce-scatter.2.cloned.1.call-done) | copy-start | bytes 1572868
  304.9 65.4 %all-to-all-start = ((f32[4,256,512]{2,1,0:T(8,128)}), f32[4,256,512]{2,1,0:T(8,128)S(1)}, u32[]{:S(2)}, u32[]{:S(2)}) async-start(f32[4,256,512]{2,1,0:T(8,128)} %bitcast.14), calls=%async_computation.1 | async-start | bytes 4194304 | tf_op jit(solution)/shard_map/all_to_all | solution.py:46
Sparse Core Ops, SparseCore 0:
  9.5 22.5 all-gather.2
  42.6 44.7 reduce-scatter.1
  89.0 44.8 all-gather.4
  136.4 18.2 all-reduce.2
where the time goes:
time: 383 us; the launch traced here: 379 us
  waiting for transfers between devices  132 us (34%)
  other arithmetic  123 us (32%)
  blocking collectives  58.8 us (15%)
  matrix products  22.1 us (6%)
  local copies, waits for them, and re-layouts  19.9 us (5%)
  between operations  18.7 us (5%)
  starting transfers between devices  4.68 us (1%)
    another operation x14, other arithmetic, local(): factor = jnp.linalg.cholesky(diag_block)  78.7 us
    psum x1, blocking collectives, local(): total = lax.psum(squares, ('row', 'col', 'depth'))  58.8 us
    all_gather x1, waiting for transfers between devices, local(): panel_block = lax.all_gather(trailing, 'depth', axis=0, tiled=True)  45.9 us
    reduce_scatter x1, waiting for transfers between devices, local(): lax.psum_scatter(jnp.where(keep_base, a_tile, 0.0) - outer_rows(panels, c...  44.9 us
    another operation x3, other arithmetic, local(): jax.scipy.linalg.solve_triangular(factor, panel_block.T, lower=True)  40.4 us
    all_gather x1, waiting for transfers between devices, local(): every_row = lax.all_gather(panels, 'row', axis=0, tiled=True)  22.2 us
    psum x1, waiting for transfers between devices, from_root(): return lax.psum(kept, axis)  18.4 us
    another operation x20, local copies, waits for them, and re-layouts  11.9 us
  transfers between devices with their start and end apart: 5, of which 4 were waited for; matrix products, arithmetic and copies ran while one was open for 1% of the time, Pallas kernels for 0%

commit v1 on v0

--- a/solution.py
+++ b/solution.py
@@ -8,7 +8,7 @@
 
 def from_root(value, axis, source):
     kept = jnp.where(lax.axis_index(axis) == source, value, 0).astype(value.dtype)
-    return lax.psum(kept, axis)
+    return jnp.sum(lax.all_gather(kept, axis), axis=0)
 
 
 def outer_rows(left, right):

time: 383 us -> 381 us (level)
  waiting for transfers between devices: 132 us -> 126 us
  matrix products: 22.1 us -> 26.5 us
    psum x1 -> x0, waiting for transfers between devices: 18.4 us -> none  [from_root(): return lax.psum(kept, axis)]
    all_gather x0 -> x1, waiting for transfers between devices: none -> 9.51 us  [from_root(): return jnp.sum(lax.all_gather(kept, axis), axis=0)]
    another operation x20 -> x12, local copies, waits for them, and re-layouts: 11.9 us -> 13.5 us
  transfers between devices with their start and end apart: 5 -> 5, of which waited for: 4 -> 4; matrix products, arithmetic and copies ran while one was open for 1% -> 0% of each run, Pallas kernels for 0% -> 0%
where the time goes in v1:
time: 381 us; the launch traced here: 377 us
  waiting for transfers between devices  126 us (33%)
  other arithmetic  125 us (33%)
  blocking collectives  58.8 us (15%)
  matrix products  26.5 us (7%)
  between operations  18.5 us (5%)
  local copies, waits for them, and re-layouts  17.7 us (5%)
  starting transfers between devices  4.67 us (1%)
    another operation x14, other arithmetic, local(): factor = jnp.linalg.cholesky(diag_block)  78.7 us
    psum x1, blocking collectives, local(): total = lax.psum(squares, ('row', 'col', 'depth'))  58.8 us
    all_gather x1, waiting for transfers between devices, local(): panel_block = lax.all_gather(trailing, 'depth', axis=0, tiled=True)  46.5 us
    reduce_scatter x1, waiting for transfers between devices, local(): lax.psum_scatter(jnp.where(keep_base, a_tile, 0.0) - outer_rows(panels, c...  44.9 us
    another operation x3, other arithmetic, local(): jax.scipy.linalg.solve_triangular(factor, panel_block.T, lower=True)  41.2 us
    all_gather x1, waiting for transfers between devices, local(): every_row = lax.all_gather(panels, 'row', axis=0, tiled=True)  24.2 us
    another operation x12, local copies, waits for them, and re-layouts  13.5 us
    another operation x7, matrix products, local(): jax.scipy.linalg.solve_triangular(factor, panel_block.T, lower=True)  10.9 us
  transfers between devices with their start and end apart: 5, of which 4 were waited for; matrix products, arithmetic and copies ran while one was open for 0% of the time, Pallas kernels for 0%

profile of v1, /device:TPU:0, one launch (start us, length us, event | category | flops | bytes accessed | tf_op | source)
XLA Modules:
  0.0 377.2 jit_solution(15728847742594490788)
XLA Ops:
  7.2 0.0 all-gather.5.cloned.1.call-start
  7.2 0.7 all-gather.5.cloned.1.call-update
  7.9 0.0 reduce-scatter.2.cloned.1.call-start
  8.0 24.2 %all-gather.5.cloned.1.call-done = f32[2048,1024]{1,0:T(8,128)} async-done(((f32[1024,1024]{1,0:T(8,128)}), f32[2048,1024]{1,0:T(8,128)}) %all-gather.5.cloned.1.call-update) | async-done | bytes 8388624 | tf_op jit(solution)/shard_map/all_gather | solution.py:31
  32.1 10.2 %bitcast_subtract_fusion = f32[1024,512]{1,0:T(8,128)} fusion(f32[1024,512]{1,0:T(8,128)S(1)} %copy-done.3, f32[1024,1024]{1,0:T(8,128)} %param.3, f32[2048,1024]{1,0:T(8,128)} %all-gather.5.cloned.1.call-done, s32[]{:T(128)S(6)} %select_n.29, pred[]{:T(512)S(6)} %eq.19), kind=kOutput, calls=%fused_computation.3 | convolution fusion | flops 6443499520 | bytes 10485765 | tf_op jit(solution)/shard_map/dot_general | solution.py:15
  42.3 0.0 reduce-scatter.2.cloned.1.call-update
  42.4 0.0 all-gather.7.cloned.1.call-start
  42.4 44.9 %reduce-scatter.2.cloned.1.call-done = f32[256,512]{1,0:T(8,128)} async-done(((f32[1024,512]{1,0:T(8,128)}), f32[256,512]{1,0:T(8,128)}) %reduce-scatter.2.cloned.1.call-update) | async-done | bytes 524304 | tf_op jit(solution)/shard_map/reduce_scatter | solution.py:35
  87.3 0.0 all-gather.7.cloned.1.call-update
  87.4 0.5 all-gather.9.cloned.1.call-start
  87.9 46.5 %all-gather.7.cloned.1.call-done = f32[1024,512]{1,0:T(8,128)} async-done(((f32[256,512]{1,0:T(8,128)}), f32[1024,512]{1,0:T(8,128)}) %all-gather.7.cloned.1.call-update) | async-done | bytes 2097168 | tf_op jit(solution)/shard_map/all_gather | solution.py:41
  134.4 2.3 slice_select_fusion
  136.7 0.0 all-gather.9.cloned.1.call-update
  136.7 9.5 %all-gather.9.cloned.1.call-done = f32[1024,512]{1,0:T(8,128)} async-done(((f32[512,512]{1,0:T(8,128)}), f32[1024,512]{1,0:T(8,128)}) %all-gather.9.cloned.1.call-update) | async-done | bytes 2097168 | tf_op jit(solution)/shard_map/all_gather | solution.py:11
  146.2 1.9 reduce_sum.18
  148.1 0.3 copy.9
  148.4 0.2 fusion.16
  148.7 1.0 copy-done.1
  149.7 11.7 %cholesky.103 = f32[128,128]{1,0:T(8,128)S(1)} custom-call(f32[128,128]{1,0:T(8,128)S(1)} %cholesky.263), custom_call_target="Cholesky" | custom-call | tf_op jit(solution)/shard_map/jit(cholesky)/cholesky | solution.py:43
  161.4 0.1 cholesky.222
  161.5 9.8 %custom-call.31 = f32[1,128,128]{1,2,0:T(8,128)S(1)} custom-call(f32[1,128,128]{2,1,0:T(8,128)S(1)} %get-tuple-element.30), custom_call_target="InvertDiagBlocksLowerTriangular" | custom-call | tf_op jit(solution)/shard_map/jit(cholesky)/cholesky | solution.py:43
  171.4 1.2 constant_dynamic-update-slice_fusion.3
  172.6 1.3 convolution_subtract_fusion.2
  173.9 11.7 %cholesky.215 = f32[128,128]{1,0:T(8,128)S(1)} custom-call(f32[128,128]{1,0:T(8,128)S(1)} %cholesky.267), custom_call_target="Cholesky" | custom-call | tf_op jit(solution)/shard_map/jit(cholesky)/cholesky | solution.py:43
  185.6 10.0 %custom-call.32 = f32[1,128,128]{1,2,0:T(8,128)S(1)} custom-call(f32[1,128,128]{2,1,0:T(8,128)S(1)} %get-tuple-element.27), custom_call_target="InvertDiagBlocksLowerTriangular" | custom-call | tf_op jit(solution)/shard_map/jit(cholesky)/cholesky | solution.py:43
  195.6 0.3 convolution_dynamic-update-slice_fusion
  195.9 1.3 convolution_subtract_fusion.3
  197.2 11.7 %cholesky.236 = f32[128,128]{1,0:T(8,128)S(1)} custom-call(f32[128,128]{1,0:T(8,128)S(1)} %cholesky.272), custom_call_target="Cholesky" | custom-call | tf_op jit(solution)/shard_map/jit(cholesky)/cholesky | solution.py:43
  208.9 0.6 compare_reduce_fusion.1
  209.5 9.8 %custom-call.33 = f32[1,128,128]{1,2,0:T(8,128)S(1)} custom-call(f32[1,128,128]{2,1,0:T(8,128)S(1)} %get-tuple-element.24), custom_call_target="InvertDiagBlocksLowerTriangular" | custom-call | tf_op jit(solution)/shard_map/jit(cholesky)/cholesky | solution.py:43
  219.3 0.2 convolution_dynamic-update-slice_fusion.1
  219.6 1.2 convolution_subtract_fusion.4
  220.8 11.9 %cholesky.253 = f32[128,128]{1,0:T(8,128)S(1)} custom-call(f32[128,128]{1,0:T(8,128)S(1)} %convolution_subtract_fusion.4), custom_call_target="Cholesky" | custom-call | tf_op jit(solution)/shard_map/jit(cholesky)/cholesky | solution.py:43
  232.7 0.7 compare_reduce_fusion
  233.4 0.7 compare_reduce_fusion.2
  236.4 1.1 select_select_fusion
  237.5 13.5 %while.1 = (s32[]{:T(128)}, f32[512,512]{1,0:T(8,128)}, s32[4,2]{0,1:T(2,128)S(1)}, f32[4,128,128]{2,1,0:T(8,128)}, s32[]{:T(128)}) while((s32[]{:T(128)}, f32[512,512]{1,0:T(8,128)}, s32[4,2]{0,1:T(2,128)S(1)}, f32[4,128,128]{2,1,0:T(8,128)}, s32[]{:T(128)}) %tuple.31), condition=%wide.while_cond, body=%wide.while_body.sunk | while | flops 2 | bytes 132205 | solution.py:44
  237.5 0.1 constant_dynamic-slice_fusion.2
  237.6 0.5 fusion.47
  238.1 2.8 bitcast_dynamic-update-slice_fusion.2
  240.9 0.1 constant_dynamic-slice_fusion.2
  241.0 0.5 fusion.47
  241.5 2.8 bitcast_dynamic-update-slice_fusion.2
  244.3 0.1 constant_dynamic-slice_fusion.2
  244.4 0.5 fusion.47
  244.9 2.8 bitcast_dynamic-update-slice_fusion.2
  247.7 0.1 constant_dynamic-slice_fusion.2
  247.8 0.5 fusion.47
  248.3 2.7 bitcast_dynamic-update-slice_fusion.2
  251.1 40.1 %custom-call.34 = f32[4,128,128]{1,2,0:T(8,128)S(1)} custom-call(f32[4,128,128]{2,1,0:T(8,128)} %get-tuple-element.10), custom_call_target="InvertDiagBlocksLowerTriangular" | custom-call | tf_op jit(solution)/shard_map/jit(_solve_triangular)/triangular_solve | solution.py:44
  291.2 0.6 fusion.17
  291.8 1.8 convolution_subtract_fusion.1
  293.7 0.6 fusion.30
  294.3 2.8 convolution_subtract_fusion
  297.1 0.6 fusion.28
  297.7 3.7 fusion.10
  301.5 0.6 fusion.27
  302.1 0.1 maximum_bitcast_fusion
  302.3 1.9 copy.12
  304.1 4.0 %all-to-all-start = ((f32[4,256,512]{2,1,0:T(8,128)}), f32[4,256,512]{2,1,0:T(8,128)S(1)}, u32[]{:S(2)}, u32[]{:S(2)}) async-start(f32[4,256,512]{2,1,0:T(8,128)} %bitcast.15), calls=%async_computation.1 | async-start | bytes 4194304 | tf_op jit(solution)/shard_map/all_to_all | solution.py:46
  308.2 0.8 select_reduce_fusion
  309.0 58.8 %psum.7 = f32[]{:T(128)} all-reduce(f32[]{:T(128)} %select_reduce_fusion), channel_id=1, replica_groups=mesh['row'=2,'col'=4,'depth'=4] {'row','col','depth'}, use_global_device_ids=true, to_apply=%region_11.12 | all-reduce | flops 1 | bytes 8 | tf_op jit(solution)/shard_map/psum | solution.py:55
  368.5 0.0 all-to-all-done
  368.5 0.8 slice_bitcast_fusion
  (19 shorter events, 0.2 us)
Async XLA Ops:
  7.2 25.0 %copy-start.3 = (f32[1024,512]{1,0:T(8,128)S(1)}, f32[1024,512]{1,0:T(8,128)}, u32[]{:S(2)}) copy-start(f32[1024,512]{1,0:T(8,128)} %param.2) | copy-start | bytes 6291460
  7.2 25.0 %all-gather.5.cloned.1.call-start = ((), (), s32[]{:S(2)}) async-start(), calls=%async_computation.2 | async-start | bytes 12582912 | tf_op jit(solution)/shard_map/all_gather | solution.py:31
  7.9 79.4 %reduce-scatter.2.cloned.1.call-start = ((), (), s32[]{:S(2)}) async-start(), calls=%async_computation.3 | async-start | bytes 2621440 | tf_op jit(solution)/shard_map/reduce_scatter | solution.py:35
  42.4 92.0 %all-gather.7.cloned.1.call-start = ((), (), s32[]{:S(2)}) async-start(), calls=%async_computation.4 | async-start | bytes 2621440 | tf_op jit(solution)/shard_map/all_gather | solution.py:41
  87.4 58.9 %all-gather.9.cloned.1.call-start = ((), (), s32[]{:S(2)}) async-start(), calls=%async_computation.5 | async-start | bytes 3145728 | tf_op jit(solution)/shard_map/all_gather | solution.py:11
  148.7 1.0 copy-start.1
  197.2 94.0 %copy-start = (f32[1024,512]{1,0:T(8,128)S(1)}, f32[1024,512]{1,0:T(8,128)}, u32[]{:S(2)}) copy-start(f32[1024,512]{1,0:T(8,128)} %all-gather.7.cloned.1.call-done) | copy-start | bytes 6291460
  304.1 4.1 %copy-start.2 = (f32[256,512]{1,0:T(8,128)S(1)}, f32[256,512]{1,0:T(8,128)}, u32[]{:S(2)}) copy-start(f32[256,512]{1,0:T(8,128)} %reduce-scatter.2.cloned.1.call-done) | copy-start | bytes 1572868
  304.1 64.4 %all-to-all-start = ((f32[4,256,512]{2,1,0:T(8,128)}), f32[4,256,512]{2,1,0:T(8,128)S(1)}, u32[]{:S(2)}, u32[]{:S(2)}) async-start(f32[4,256,512]{2,1,0:T(8,128)} %bitcast.15), calls=%async_computation.1 | async-start | bytes 4194304 | tf_op jit(solution)/shard_map/all_to_all | solution.py:46
Sparse Core Ops, SparseCore 0:
  9.5 22.5 all-gather.4
  42.5 44.7 reduce-scatter.1
  89.5 44.8 all-gather.6
  136.8 9.3 all-gather.8
